TPU v7x, 32 devices: a whole 2x2x4 slice. The times are simulated.
32 devices in a mesh: ty: 4 (over z), tx: 8 (over y, x, core).
Axes of the slice: x: 2, y: 2, z: 4, core: 2. Of those that a mesh axis runs over, the one named last changes fastest.
Arguments:
- object_slices: float32 [2, 2, 2048, 4096], P(None, None, 'ty', 'tx'), may hold values from -4 to 4
- probe_modes: float32 [4, 2, 128, 128], replicated, may hold values from -12 to 12
- patterns: bfloat16 [256, 128, 128], P(('ty', 'tx')), may hold values from 0 to 2
- positions: int32 [256, 2], replicated, may hold values from 0 to 4095, as said below
- counts: int32 [32], replicated, may hold values from 6 to 8, as said below
Outputs:
- new_object: float32 [2, 2, 2048, 4096], P(None, None, 'ty', 'tx')
- new_probe: float32 [4, 2, 128, 128], replicated
Inputs may be any that keep to these rules, and one draw needn't show every extreme that they name: positions[j] is the centre of pattern j, which was acquired by device j // 8 of ty+tx (ty slowest); its column lies in that device's column of tiles of 512 x 512 cells. Of the live patterns of one device, at most 2 lie in any one row of tiles; in every column of tiles some row of tiles holds exactly 2 live patterns from every device of that column. The live patterns of device d are its first counts[d] slots; some device has 8.
All inputs are finite; a program needn't handle non-finite values.
Results may differ from a plain program's by a relative error of at most 0.0085.
The roundings to bfloat16 on the way count: a program that leaves them out, or rounds other values in their place, can miss the bound.
Values may be sent and summed in bfloat16 or wider, within the bound.
No kernel may reach another device: no remote copies, remote signals or barrier semaphores. Data moves between devices by JAX's collectives and lax.ppermute only.
A program may use at most 128 MiB of HBM per device.

v0:
```python
import math
import jax
import jax.numpy as jnp
from jax import lax
from jax.sharding import PartitionSpec as P

CAP = 2
PROPAGATION = 0.37


def extended_2(block, sides, width):
    for axis, dim in sides:
        count = lax.axis_size(axis)
        forward = [(i, i + 1) for i in range(count - 1)]
        backward = [(target, source) for source, target in forward]
        low = lax.ppermute(
            lax.slice_in_dim(block, block.shape[dim] - width, None, axis=dim), axis, forward
        )
        high = lax.ppermute(lax.slice_in_dim(block, 0, width, axis=dim), axis, backward)
        block = jnp.concatenate([low, block, high], axis=dim)
    return block


def make_tables(extent):
    indices = jnp.arange(extent, dtype=jnp.int32)
    product = indices[:, None] * indices[None, :] % extent
    angles = 2.0 * jnp.pi / extent * product.astype(jnp.float32)
    norm_scale = 1.0 / math.sqrt(extent)
    real_table = (jnp.cos(angles) * norm_scale).astype(jnp.bfloat16)
    imag_table = (-jnp.sin(angles) * norm_scale).astype(jnp.bfloat16)
    right_fwd = jnp.concatenate(
        [
            jnp.concatenate([real_table, imag_table], 1),
            jnp.concatenate([-imag_table, real_table], 1),
        ],
        0,
    )
    right_inv = jnp.concatenate(
        [
            jnp.concatenate([real_table, -imag_table], 1),
            jnp.concatenate([imag_table, real_table], 1),
        ],
        0,
    )
    left_fwd = jnp.concatenate([real_table, imag_table], 0)
    left_inv = jnp.concatenate([real_table, -imag_table], 0)
    frequency = jnp.where(indices < extent // 2, indices, indices - extent).astype(jnp.float32)
    phases = -jnp.pi * PROPAGATION / extent * (frequency[:, None] ** 2 + frequency[None, :] ** 2)
    kernel = jnp.stack([jnp.cos(phases), jnp.sin(phases)])
    return (right_fwd, left_fwd, right_inv, left_inv, kernel)


def transform(wave_field, right_table, left_table):
    extent = wave_field.shape[-1]
    rounded = wave_field.astype(jnp.bfloat16)
    joined = jnp.concatenate([rounded[:, 0], rounded[:, 1]], axis=-1)
    partial_value = jnp.einsum(
        "bpk,kq->bpq", joined, right_table, preferred_element_type=jnp.float32
    ).astype(jnp.bfloat16)
    stacked = jnp.einsum(
        "ij,bjq->biq", left_table, partial_value, preferred_element_type=jnp.float32
    )
    real_part = stacked[:, :extent, :extent] - stacked[:, extent:, extent:]
    imag_part = stacked[:, extent:, :extent] + stacked[:, :extent, extent:]
    return jnp.stack([real_part, imag_part], axis=1)


def complex_product(former, latter):
    former_re = former[..., 0, :, :]
    former_im = former[..., 1, :, :]
    latter_re = latter[..., 0, :, :]
    latter_im = latter[..., 1, :, :]
    return jnp.stack(
        [
            former_re * latter_re - former_im * latter_im,
            former_re * latter_im + former_im * latter_re,
        ],
        axis=-3,
    )


def conjugate(values):
    return jnp.stack([values[..., 0, :, :], -values[..., 1, :, :]], axis=-3)


def pattern_terms(window, amplitude, live_flag, probe_modes, tables):
    right_fwd, left_fwd, right_inv, left_inv, kernel = tables
    slices = window.shape[0]
    inputs = [probe_modes]
    far_field = None
    for slice_index in range(slices):
        exit_wave = complex_product(inputs[slice_index], window[slice_index])
        if slice_index + 1 < slices:
            spread_wave = complex_product(kernel, transform(exit_wave, right_fwd, left_fwd))
            inputs.append(transform(spread_wave, right_inv, left_inv))
        else:
            far_field = transform(exit_wave, right_fwd, left_fwd)
    intensity = jnp.sum(far_field[:, 0] ** 2 + far_field[:, 1] ** 2, axis=0)
    factor = (1.0 - amplitude / jnp.sqrt(jnp.maximum(intensity, 0.25))) * live_flag
    residue = far_field * factor
    backward = transform(residue, right_inv, left_inv)
    slice_grads = [None] * slices
    for slice_index in reversed(range(slices)):
        slice_grads[slice_index] = jnp.sum(
            complex_product(conjugate(inputs[slice_index]), backward), axis=0
        )
        if slice_index > 0:
            inner_wave = transform(
                complex_product(conjugate(window[slice_index]), backward), right_fwd, left_fwd
            )
            backward = transform(
                complex_product(conjugate(kernel), inner_wave), right_inv, left_inv
            )
    probe_term = complex_product(conjugate(window[0]), backward)
    return (jnp.stack(slice_grads), probe_term)


def settle(centre, leading, trailing, axis, margin):
    length = centre.shape[axis]
    top_part = lax.slice_in_dim(centre, 0, margin, axis=axis) + leading
    middle_part = lax.slice_in_dim(centre, margin, length - margin, axis=axis)
    bottom_part = lax.slice_in_dim(centre, length - margin, length, axis=axis) + trailing
    return jnp.concatenate([top_part, middle_part, bottom_part], axis=axis)


def on_device(object_slices, probe_modes, patterns, positions, counts):
    slices = object_slices.shape[0]
    tile_cells = object_slices.shape[2]
    extent = probe_modes.shape[-1]
    margin = extent // 2
    per_device = patterns.shape[0]
    row_count = lax.axis_size("ty")
    column_count = lax.axis_size("tx")
    row_index = lax.axis_index("ty")
    column_index = lax.axis_index("tx")
    position_grid = positions.reshape(row_count, column_count, per_device, 2)
    column = lax.dynamic_index_in_dim(position_grid, column_index, axis=1, keepdims=False)
    count_grid = counts.reshape(row_count, column_count)
    column_counts = lax.dynamic_index_in_dim(count_grid, column_index, axis=1, keepdims=False)
    ordinal = jnp.arange(per_device, dtype=jnp.int32)
    is_live = ordinal[None, :] < column_counts[:, None]
    target = column[:, :, 0] // tile_cells
    earlier = ordinal[None, :] < ordinal[:, None]
    same_row = is_live[:, None, :] & (target[:, None, :] == target[:, :, None]) & earlier[None]
    row_rank = jnp.sum(same_row.astype(jnp.int32), axis=2)
    slot_count = row_count * CAP
    slot_ids = jnp.arange(slot_count, dtype=jnp.int32)
    own_live = lax.dynamic_index_in_dim(is_live, row_index, axis=0, keepdims=False)
    own_slot = lax.dynamic_index_in_dim(target * CAP + row_rank, row_index, axis=0, keepdims=False)
    choose = (own_live[None, :] & (own_slot[None, :] == slot_ids[:, None])).astype(jnp.bfloat16)
    outgoing = jnp.einsum(
        "sj,jab->sab", choose, patterns, preferred_element_type=jnp.float32
    ).astype(jnp.bfloat16)
    incoming = lax.all_to_all(outgoing, "ty", split_axis=0, concat_axis=0, tiled=True)
    rank_ids = jnp.arange(CAP, dtype=jnp.int32)
    matched = (
        is_live[:, None, :]
        & (target[:, None, :] == row_index)
        & (row_rank[:, None, :] == rank_ids[None, :, None])
    )
    slot_live = jnp.any(matched, axis=2).reshape(-1)
    chosen = matched.astype(jnp.int32)
    centre_row = jnp.sum(chosen * column[:, None, :, 0], axis=2).reshape(-1)
    centre_col = jnp.sum(chosen * column[:, None, :, 1], axis=2).reshape(-1)
    local_row = jnp.where(slot_live, centre_row - row_index * tile_cells, 0)
    local_col = jnp.where(slot_live, centre_col - column_index * tile_cells, 0)
    extended = extended_2(object_slices, (("ty", 2), ("tx", 3)), margin)
    tables = make_tables(extent)

    def visit_slot(running, element):
        gradient, probe_grad = running
        amplitude, row_start, col_start, live_flag = element
        corner = (jnp.int32(0), jnp.int32(0), row_start, col_start)
        window = lax.dynamic_slice(extended, corner, (slices, 2, extent, extent))
        slice_grads, probe_term = pattern_terms(
            window, amplitude.astype(jnp.float32), live_flag, probe_modes, tables
        )
        current = lax.dynamic_slice(gradient, corner, (slices, 2, extent, extent))
        gradient = lax.dynamic_update_slice(gradient, current + slice_grads, corner)
        return ((gradient, probe_grad + probe_term), None)

    span_cells = tile_cells + extent
    initial = (
        jnp.zeros((slices, 2, span_cells, span_cells), jnp.float32),
        jnp.zeros(probe_modes.shape, jnp.float32),
    )
    (gradient, probe_grad), unused = lax.scan(
        visit_slot, initial, (incoming, local_row, local_col, slot_live.astype(jnp.float32))
    )
    row_edges = jnp.concatenate([gradient[:, :, :margin], gradient[:, :, -margin:]], axis=2)
    row_halo = extended_2(row_edges, (("ty", 2),), margin)
    row_folded = settle(
        gradient[:, :, margin : margin + tile_cells],
        row_halo[:, :, :margin],
        row_halo[:, :, -margin:],
        2,
        margin,
    )
    col_edges = jnp.concatenate([row_folded[..., :margin], row_folded[..., -margin:]], axis=3)
    col_halo = extended_2(col_edges, (("tx", 3),), margin)
    folded = settle(
        row_folded[..., margin : margin + tile_cells],
        col_halo[..., :margin],
        col_halo[..., -margin:],
        3,
        margin,
    )
    probe_power = jnp.mean(jnp.sum(probe_modes**2, axis=(0, 1)))
    new_object = object_slices - folded / (probe_power + 1e-06)
    summed = lax.psum(probe_grad, ("ty", "tx"))
    spread = jnp.sqrt(jnp.mean(summed * summed) + 1e-06)
    new_probe = probe_modes - 0.5 * summed / spread
    return (new_object, new_probe)


def solution(mesh):
    return jax.shard_map(
        on_device,
        mesh=mesh,
        in_specs=(P(None, None, "ty", "tx"), P(), P(("ty", "tx"), None, None), P(), P()),
        out_specs=(P(None, None, "ty", "tx"), P()),
        check_vma=False,
    )
```

profile of v0, /device:TPU:0, one launch (start us, length us, event | category | flops | bytes accessed | tf_op | source)
XLA Modules:
  0.0 498.1 jit_solution(16212770416473145393)
XLA Ops:
  10.3 6.3 %all-to-all-start = ((bf16[8,128,128]{2,1,0:T(8,128)(2,1)}), bf16[8,128,128]{2,1,0:T(8,128)(2,1)}, u32[]{:S(2)}, u32[]{:S(2)}) async-start(bf16[8,128,128]{2,1,0:T(8,128)(2,1)} %copy.108), calls=%async_computation | async-start | bytes 524288 | tf_op jit(solution)/shard_map/all_to_all | solution.py:154
  18.0 4.0 collective-permute-start
  23.2 5.2 %copy.120 = f32[2,2,512,512]{2,3,1,0:T(8,128)} copy(f32[2,2,512,512]{3,2,1,0:T(8,128)} %param.7) | data formatting | bytes 8388608 | tf_op args[0]
  30.5 2.0 collective-permute-done
  32.8 4.0 collective-permute-done.1
  37.2 2.8 pad_maximum_fusion.4
  40.0 2.1 collective-permute-start.2
  47.4 5.9 %pad_maximum_fusion = f32[2,2,640,640]{2,3,1,0:T(8,128)} fusion(f32[2,2,640,64]{2,3,1,0:T(8,128)} %collective-permute-done.3, f32[2,2,64,512]{2,3,1,0:T(8,128)S(1)} %copy.106, f32[2,2,512,512]{2,3,1,0:T(8,128)} %copy.120, f32[2,2,64,512]{2,3,1,0:T(8,128)S(1)} %copy.104, f32[2,2,640,64]{2,3,1,0:T(8,128)} %collective-permute-done.2), kind=kLoop, calls=%fused_computation.110 | loop fusion | flops 6553600 | bytes 13107200 | tf_op jit(solution)/shard_map/concatenate | solution.py:20
  53.3 3.2 broadcast_in_dim.8
  56.5 217.4 %while.18 = (s32[]{:T(128)}, f32[2,2,640,640]{2,3,1,0:T(8,128)}, f32[4,2,128,128]{3,2,0,1:T(8,128)S(1)}, s32[8]{0:T(128)S(1)}, s32[8]{0:T(128)S(1)}, /*index=5*/...) while((s32[]{:T(128)}, f32[2,2,640,640]{2,3,1,0:T(8,128)}, ...), condition=%wide.region_8.9_spmd.clone.clone.clone.clone, body=%wide.region_4.8_spmd.clone.clone.clone.clone.sunk | while | flops 815677440 | bytes 33391468 | solution.py:187
  67.7 1.5 convolution_bitcast_fusion.13
  70.0 1.5 convolution_bitcast_fusion.14
  71.5 1.5 fusion.155
  73.7 1.5 convolution_bitcast_fusion.15
  79.3 4.4 dynamic_update_slice.10
  94.9 1.5 convolution_bitcast_fusion.13
  97.1 1.5 convolution_bitcast_fusion.14
  100.9 1.5 convolution_bitcast_fusion.15
  106.5 4.2 dynamic_update_slice.10
  121.9 1.5 convolution_bitcast_fusion.13
  124.2 1.5 convolution_bitcast_fusion.14
  127.9 1.5 convolution_bitcast_fusion.15
  133.5 4.4 dynamic_update_slice.10
  149.1 1.5 convolution_bitcast_fusion.13
  151.4 1.5 convolution_bitcast_fusion.14
  152.9 1.5 fusion.155
  155.1 1.5 convolution_bitcast_fusion.15
  160.7 4.4 dynamic_update_slice.10
  176.3 1.5 convolution_bitcast_fusion.13
  178.6 1.5 convolution_bitcast_fusion.14
  182.3 1.5 convolution_bitcast_fusion.15
  187.9 4.4 dynamic_update_slice.10
  203.5 1.5 convolution_bitcast_fusion.13
  205.7 1.5 convolution_bitcast_fusion.14
  209.5 1.5 convolution_bitcast_fusion.15
  215.1 4.3 dynamic_update_slice.10
  230.6 1.5 convolution_bitcast_fusion.13
  232.9 1.5 convolution_bitcast_fusion.14
  236.6 1.5 convolution_bitcast_fusion.15
  242.2 4.4 dynamic_update_slice.10
  257.8 1.5 convolution_bitcast_fusion.13
  260.1 1.5 convolution_bitcast_fusion.14
  263.9 1.5 convolution_bitcast_fusion.15
  269.4 4.4 dynamic_update_slice.10
  273.8 8.2 %copy.114 = f32[2,2,640,640]{3,2,1,0:T(8,128)} copy(f32[2,2,640,640]{2,3,1,0:T(8,128)} %get-tuple-element.206) | data formatting | bytes 13107200 | tf_op jit(solution)/shard_map/while | solution.py:187
  283.1 1.9 collective-permute-start.4
  285.0 8.0 %collective-permute-done.4 = f32[2,2,64,640]{3,2,1,0:T(8,128)S(1)} collective-permute-done((f32[2,2,64,640]{3,2,1,0:T(8,128)S(1)}, f32[2,2,64,640]{3,2,1,0:T(8,128)S(1)}, u32[]{:S(2)}, u32[]{:S(2)}) %collective-permute-start.4) | collective-permute-done | bytes 655392 | tf_op jit(solution)/shard_map/ppermute | solution.py:16
  293.1 2.3 slice_add_fusion.7
  295.3 1.5 collective-permute-start.5
  296.8 4.2 slice.281
  301.4 7.1 %collective-permute-done.5 = f32[2,2,64,640]{3,2,1,0:T(8,128)S(1)} collective-permute-done((f32[2,2,64,640]{3,2,1,0:T(8,128)}, f32[2,2,64,640]{3,2,1,0:T(8,128)S(1)}, u32[]{:S(2)}, u32[]{:S(2)}) %collective-permute-start.5) | collective-permute-done | bytes 655392 | tf_op jit(solution)/shard_map/ppermute | solution.py:19
  308.5 2.0 slice_add_fusion.6
  310.5 1.5 copy.119
  312.0 2.0 pad_maximum_fusion.6
  314.0 14.0 %collective-permute-start.6 = (f32[2,2,512,64]{2,3,1,0:T(8,128)}, f32[2,2,512,64]{2,3,1,0:T(8,128)}, u32[]{:S(2)}, u32[]{:S(2)}) collective-permute-start(f32[2,2,512,64]{2,3,1,0:T(8,128)} %pad_maximum_fusion.6), channel_id=1, source_target_pairs={{0,1},{1,2},{2,3},{3,4},{4,5},{5,6},{6,7},{8,9},{9,10},{10,11},{11... | collective-permute-start | bytes 1572872 | tf_op jit(solution)/shard_map/ppermute | solution.py:16
  329.1 2.7 maximum_add_fusion.3
  333.0 136.7 %all-reduce.2.cloned.1.call-done = f32[4,2,128,128]{3,2,1,0:T(8,128)} async-done(((f32[4,2,128,128]{3,2,1,0:T(8,128)}), f32[4,2,128,128]{3,2,1,0:T(8,128)}) %all-reduce.2.cloned.1.call-update) | async-done | bytes 524304 | tf_op jit(solution)/shard_map/psum | solution.py:210
  469.7 1.8 multiply_reduce_fusion
  472.2 2.5 divide_subtract_fusion
  475.4 3.9 pad_maximum_fusion.1
  479.6 1.8 copy-done.2
  481.4 1.7 maximum_add_fusion.2
  483.1 3.0 fusion.85
  486.1 5.2 %copy.122 = f32[2,2,512,512]{3,2,1,0:T(8,128)} copy(f32[2,2,512,512]{2,3,1,0:T(8,128)} %fusion.85) | data formatting | bytes 8388608
  (355 shorter events, 128.7 us)
Async XLA Ops:
  7.2 2.1 copy-start
  10.3 43.0 %all-to-all-start = ((bf16[8,128,128]{2,1,0:T(8,128)(2,1)}), bf16[8,128,128]{2,1,0:T(8,128)(2,1)}, u32[]{:S(2)}, u32[]{:S(2)}) async-start(bf16[8,128,128]{2,1,0:T(8,128)(2,1)} %copy.108), calls=%async_computation | async-start | bytes 524288 | tf_op jit(solution)/shard_map/all_to_all | solution.py:154
  16.7 453.1 %all-reduce.2.cloned.1.call-start = ((), (), s32[]{:S(2)}) async-start(), calls=%async_computation.1 | async-start | bytes 1048576 | tf_op jit(solution)/shard_map/psum | solution.py:210
  18.0 14.5 %collective-permute-start = (f32[2,2,64,512]{3,2,1,0:T(8,128)S(1)}, f32[2,2,64,512]{3,2,1,0:T(8,128)S(1)}, u32[]{:S(2)}, u32[]{:S(2)}) collective-permute-start(f32[2,2,64,512]{3,2,1,0:T(8,128)S(1)} %get-tuple-element.545), channel_id=1, source_target_pairs={{0,8},{8,16},{16,24},{1,9},{9,17},{17,25},{2,10},{10,18},{18,26},{... | collective-permute-start | bytes 1572872 | tf_op jit(solution)/shard_map/ppermute | solution.py:16
  21.9 14.9 %collective-permute-start.1 = (f32[2,2,64,512]{3,2,1,0:T(8,128)S(1)}, f32[2,2,64,512]{3,2,1,0:T(8,128)S(1)}, u32[]{:S(2)}, u32[]{:S(2)}) collective-permute-start(f32[2,2,64,512]{3,2,1,0:T(8,128)S(1)} %get-tuple-element.546), channel_id=1, source_target_pairs={{8,0},{16,8},{24,16},{9,1},{17,9},{25,17},{10,2},{18,10},{26,18},{... | collective-permute-start | bytes 1572872 | tf_op jit(solution)/shard_map/ppermute | solution.py:19
  29.6 0.6 copy-start.8
  29.8 0.6 copy-start.10
  29.9 0.6 copy-start.12
  37.1 6.3 %copy-start.9 = (bf16[128,128]{1,0:T(8,128)(2,1)S(1)}, bf16[128,128]{1,0:T(8,128)(2,1)}, u32[]{:S(2)}) copy-start(bf16[128,128]{1,0:T(8,128)(2,1)} %copy-done.8) | copy-start | bytes 98308
  37.2 6.3 %copy-start.11 = (bf16[128,128]{1,0:T(8,128)(2,1)S(1)}, bf16[128,128]{1,0:T(8,128)(2,1)}, u32[]{:S(2)}) copy-start(bf16[128,128]{1,0:T(8,128)(2,1)} %copy-done.10) | copy-start | bytes 98308
  37.2 6.3 %copy-start.13 = (bf16[128,128]{1,0:T(8,128)(2,1)S(1)}, bf16[128,128]{1,0:T(8,128)(2,1)}, u32[]{:S(2)}) copy-start(bf16[128,128]{1,0:T(8,128)(2,1)} %copy-done.12) | copy-start | bytes 98308
  37.2 6.3 %copy-start.14 = (pred[4,2]{0,1:T(4,128)(4,1)S(1)}, pred[4,2]{0,1:T(4,128)(4,1)}, u32[]{:S(2)}) copy-start(pred[4,2]{0,1:T(4,128)(4,1)} %reduce_or.9) | copy-start | bytes 28
  37.2 6.3 %copy-start.5 = (f32[4,2,128,128]{3,2,1,0:T(8,128)S(1)}, f32[4,2,128,128]{3,2,1,0:T(8,128)}, u32[]{:S(2)}) copy-start(f32[4,2,128,128]{3,2,1,0:T(8,128)} %param.8) | copy-start | bytes 1572868
  40.0 6.6 %collective-permute-start.2 = (f32[2,2,640,64]{2,3,1,0:T(8,128)}, f32[2,2,640,64]{2,3,1,0:T(8,128)}, u32[]{:S(2)}, u32[]{:S(2)}) collective-permute-start(f32[2,2,640,64]{2,3,1,0:T(8,128)} %get-tuple-element.543), channel_id=1, source_target_pairs={{0,1},{1,2},{2,3},{3,4},{4,5},{5,6},{6,7},{8,9},{9,10},{10,11},{11... | collective-permute-start | bytes 1966088 | tf_op jit(solution)/shard_map/ppermute | solution.py:16
  42.1 5.2 %collective-permute-start.3 = (f32[2,2,640,64]{2,3,1,0:T(8,128)}, f32[2,2,640,64]{2,3,1,0:T(8,128)}, u32[]{:S(2)}, u32[]{:S(2)}) collective-permute-start(f32[2,2,640,64]{2,3,1,0:T(8,128)} %get-tuple-element.544), channel_id=1, source_target_pairs={{1,0},{2,1},{3,2},{4,3},{5,4},{6,5},{7,6},{9,8},{10,9},{11,10},{12... | collective-permute-start | bytes 1966088 | tf_op jit(solution)/shard_map/ppermute | solution.py:19
  53.3 3.2 copy-start.15
  75.3 2.3 copy-start.4
  102.5 2.3 copy-start.4
  129.5 2.3 copy-start.4
  156.7 2.3 copy-start.4
  183.9 2.3 copy-start.4
  211.1 2.3 copy-start.4
  238.2 2.3 copy-start.4
  265.5 2.3 copy-start.4
  283.1 9.9 %collective-permute-start.4 = (f32[2,2,64,640]{3,2,1,0:T(8,128)S(1)}, f32[2,2,64,640]{3,2,1,0:T(8,128)S(1)}, u32[]{:S(2)}, u32[]{:S(2)}) collective-permute-start(f32[2,2,64,640]{3,2,1,0:T(8,128)S(1)} %slice.455), channel_id=1, source_target_pairs={{0,8},{8,16},{16,24},{1,9},{9,17},{17,25},{2,10},{10,18},{18,26},{... | collective-permute-start | bytes 1966088 | tf_op jit(solution)/shard_map/ppermute | solution.py:16
  295.3 13.1 %collective-permute-start.5 = (f32[2,2,64,640]{3,2,1,0:T(8,128)}, f32[2,2,64,640]{3,2,1,0:T(8,128)S(1)}, u32[]{:S(2)}, u32[]{:S(2)}) collective-permute-start(f32[2,2,64,640]{3,2,1,0:T(8,128)} %get-tuple-element.542), channel_id=1, source_target_pairs={{8,0},{16,8},{24,16},{9,1},{17,9},{25,17},{10,2},{18,10},{26,18},{... | collective-permute-start | bytes 1966088 | tf_op jit(solution)/shard_map/ppermute | solution.py:19
  314.0 15.1 %collective-permute-start.6 = (f32[2,2,512,64]{2,3,1,0:T(8,128)}, f32[2,2,512,64]{2,3,1,0:T(8,128)}, u32[]{:S(2)}, u32[]{:S(2)}) collective-permute-start(f32[2,2,512,64]{2,3,1,0:T(8,128)} %pad_maximum_fusion.6), channel_id=1, source_target_pairs={{0,1},{1,2},{2,3},{3,4},{4,5},{5,6},{6,7},{8,9},{9,10},{10,11},{11... | collective-permute-start | bytes 1572872 | tf_op jit(solution)/shard_map/ppermute | solution.py:16
  328.9 143.3 %copy-start.6 = (f32[4,2,128,128]{3,2,1,0:T(8,128)S(1)}, f32[4,2,128,128]{3,2,1,0:T(8,128)}, u32[]{:S(2)}) copy-start(f32[4,2,128,128]{3,2,1,0:T(8,128)} %param.8) | copy-start | bytes 1572868
  331.7 147.9 %collective-permute-start.7 = (f32[2,2,512,64]{2,3,1,0:T(8,128)}, f32[2,2,512,64]{2,3,1,0:T(8,128)}, u32[]{:S(2)}, u32[]{:S(2)}) collective-permute-start(f32[2,2,512,64]{2,3,1,0:T(8,128)} %get-tuple-element.540), channel_id=1, source_target_pairs={{1,0},{2,1},{3,2},{4,3},{5,4},{6,5},{7,6},{9,8},{10,9},{11,10},{12... | collective-permute-start | bytes 1572872 | tf_op jit(solution)/shard_map/ppermute | solution.py:19
  479.3 2.1 copy-start.2
  479.6 3.5 copy-start.3
  479.6 3.5 copy-start.7
  483.1 8.2 %copy-start.1 = (bf16[8,128,128]{2,1,0:T(8,128)(2,1)S(1)}, bf16[8,128,128]{2,1,0:T(8,128)(2,1)}, u32[]{:S(2)}) copy-start(bf16[8,128,128]{2,1,0:T(8,128)(2,1)} %param.9) | copy-start | bytes 786436
Sparse Core Ops, SparseCore 0:
  329.0 140.7 all-reduce.1
where the time goes:
time: 503 us; the launch traced here: 498 us
  waiting for transfers between devices  159 us (32%)
  local copies, waits for them, and re-layouts  119 us (24%)
  other arithmetic  88.5 us (18%)
  matrix products  49.7 us (10%)
  starting transfers between devices  33.7 us (7%)
  loops' own time  32.6 us (6%)
  between operations  15.8 us (3%)
    psum x1, waiting for transfers between devices, on_device(): summed = lax.psum(probe_grad, ('ty', 'tx'))  137 us
    dot_general x48, matrix products, transform(): jnp.einsum('ij,bjq->biq', left_table, partial_value, preferred_element_ty...  49.5 us
    dynamic_update_slice x8, local copies, waits for them, and re-layouts, visit_slot(): gradient = lax.dynamic_update_slice(gradient, current + slice_grads, corner)  34.9 us
    another operation x1, loops' own time, on_device(): lax.scan(visit_slot, initial, (incoming, local_row, local_col, slot_live....  32.6 us
    dynamic_slice x40, local copies, waits for them, and re-layouts, on_device(): lax.scan(visit_slot, initial, (incoming, local_row, local_col, slot_live....  26.4 us
    ppermute x4, starting transfers between devices, extended_2(): lax.ppermute(lax.slice_in_dim(block, block.shape[dim] - width, None, axis...  22 us
    squeeze x48, other arithmetic, transform(): joined = jnp.concatenate([rounded[:, 0], rounded[:, 1]], axis=-1)  20.9 us
    unnamed x33, local copies, waits for them, and re-layouts  12.9 us
  transfers between devices with their start and end apart: 10, of which 7 were waited for; matrix products, arithmetic and copies ran while one was open for 7% of the time, Pallas kernels for 0%

commit v1 on v0

--- a/solution.py
+++ b/solution.py
@@ -207,7 +207,9 @@
     )
     probe_power = jnp.mean(jnp.sum(probe_modes**2, axis=(0, 1)))
     new_object = object_slices - folded / (probe_power + 1e-06)
-    summed = lax.psum(probe_grad, ("ty", "tx"))
+    summed = probe_grad
+    for name in ("tx", "ty"):
+        summed = lax.psum(summed, name)
     spread = jnp.sqrt(jnp.mean(summed * summed) + 1e-06)
     new_probe = probe_modes - 0.5 * summed / spread
     return (new_object, new_probe)

time: 503 us -> 469 us (0.932)
  waiting for transfers between devices: 159 us -> 125 us
    psum x1 -> x2, waiting for transfers between devices: 137 us -> 103 us  [on_device(): summed = lax.psum(summed, name)]
  transfers between devices with their start and end apart: 10 -> 11, of which waited for: 7 -> 7; matrix products, arithmetic and copies ran while one was open for 7% -> 8% of each run, Pallas kernels for 0% -> 0%
where the time goes in v1:
time: 469 us; the launch traced here: 464 us
  waiting for transfers between devices  125 us (27%)
  local copies, waits for them, and re-layouts  119 us (25%)
  other arithmetic  88.6 us (19%)
  matrix products  49.7 us (11%)
  starting transfers between devices  33.7 us (7%)
  loops' own time  32.6 us (7%)
  between operations  15.8 us (3%)
    psum x2, waiting for transfers between devices, on_device(): summed = lax.psum(summed, name)  103 us
    dot_general x48, matrix products, transform(): jnp.einsum('ij,bjq->biq', left_table, partial_value, preferred_element_ty...  49.5 us
    dynamic_update_slice x8, local copies, waits for them, and re-layouts, visit_slot(): gradient = lax.dynamic_update_slice(gradient, current + slice_grads, corner)  34.9 us
    another operation x1, loops' own time, on_device(): lax.scan(visit_slot, initial, (incoming, local_row, local_col, slot_live....  32.6 us
    dynamic_slice x40, local copies, waits for them, and re-layouts, on_device(): lax.scan(visit_slot, initial, (incoming, local_row, local_col, slot_live....  26.4 us
    ppermute x4, starting transfers between devices, extended_2(): lax.ppermute(lax.slice_in_dim(block, block.shape[dim] - width, None, axis...  22 us
    squeeze x48, other arithmetic, transform(): joined = jnp.concatenate([rounded[:, 0], rounded[:, 1]], axis=-1)  20.9 us
    unnamed x33, local copies, waits for them, and re-layouts  12.9 us
  transfers between devices with their start and end apart: 11, of which 7 were waited for; matrix products, arithmetic and copies ran while one was open for 8% of the time, Pallas kernels for 0%

profile of v1, /device:TPU:0, one launch (start us, length us, event | category | flops | bytes accessed | tf_op | source)
XLA Modules:
  0.0 464.2 jit_solution(6345001081023153027)
XLA Ops:
  10.3 6.3 %all-to-all-start = ((bf16[8,128,128]{2,1,0:T(8,128)(2,1)}), bf16[8,128,128]{2,1,0:T(8,128)(2,1)}, u32[]{:S(2)}, u32[]{:S(2)}) async-start(bf16[8,128,128]{2,1,0:T(8,128)(2,1)} %copy.108), calls=%async_computation | async-start | bytes 524288 | tf_op jit(solution)/shard_map/all_to_all | solution.py:154
  18.0 4.0 collective-permute-start
  23.2 5.2 %copy.120 = f32[2,2,512,512]{2,3,1,0:T(8,128)} copy(f32[2,2,512,512]{3,2,1,0:T(8,128)} %param.7) | data formatting | bytes 8388608 | tf_op args[0]
  30.5 2.0 collective-permute-done
  32.8 4.0 collective-permute-done.1
  37.2 2.8 pad_maximum_fusion.4
  40.0 2.1 collective-permute-start.2
  47.4 5.9 %pad_maximum_fusion = f32[2,2,640,640]{2,3,1,0:T(8,128)} fusion(f32[2,2,640,64]{2,3,1,0:T(8,128)} %collective-permute-done.3, f32[2,2,64,512]{2,3,1,0:T(8,128)S(1)} %copy.106, f32[2,2,512,512]{2,3,1,0:T(8,128)} %copy.120, f32[2,2,64,512]{2,3,1,0:T(8,128)S(1)} %copy.104, f32[2,2,640,64]{2,3,1,0:T(8,128)} %collective-permute-done.2), kind=kLoop, calls=%fused_computation.110 | loop fusion | flops 6553600 | bytes 13107200 | tf_op jit(solution)/shard_map/concatenate | solution.py:20
  53.3 3.2 broadcast_in_dim.8
  56.5 217.4 %while.18 = (s32[]{:T(128)}, f32[2,2,640,640]{2,3,1,0:T(8,128)}, f32[4,2,128,128]{3,2,0,1:T(8,128)S(1)}, s32[8]{0:T(128)S(1)}, s32[8]{0:T(128)S(1)}, /*index=5*/...) while((s32[]{:T(128)}, f32[2,2,640,640]{2,3,1,0:T(8,128)}, ...), condition=%wide.region_8.9_spmd.clone.clone.clone.clone, body=%wide.region_4.8_spmd.clone.clone.clone.clone.sunk | while | flops 815677440 | bytes 33391468 | solution.py:187
  67.7 1.5 convolution_bitcast_fusion.13
  70.0 1.5 convolution_bitcast_fusion.14
  73.7 1.5 convolution_bitcast_fusion.15
  79.3 4.4 dynamic_update_slice.10
  94.9 1.5 convolution_bitcast_fusion.13
  97.1 1.5 convolution_bitcast_fusion.14
  100.9 1.5 convolution_bitcast_fusion.15
  106.5 4.2 dynamic_update_slice.10
  121.9 1.5 convolution_bitcast_fusion.13
  124.2 1.5 convolution_bitcast_fusion.14
  127.9 1.5 convolution_bitcast_fusion.15
  133.5 4.4 dynamic_update_slice.10
  149.1 1.5 convolution_bitcast_fusion.13
  151.4 1.5 convolution_bitcast_fusion.14
  152.9 1.5 fusion.155
  155.1 1.5 convolution_bitcast_fusion.15
  160.7 4.4 dynamic_update_slice.10
  176.3 1.5 convolution_bitcast_fusion.13
  178.6 1.5 convolution_bitcast_fusion.14
  182.3 1.5 convolution_bitcast_fusion.15
  187.9 4.4 dynamic_update_slice.10
  203.5 1.5 convolution_bitcast_fusion.13
  205.7 1.5 convolution_bitcast_fusion.14
  209.5 1.5 convolution_bitcast_fusion.15
  215.1 4.3 dynamic_update_slice.10
  230.6 1.5 convolution_bitcast_fusion.13
  232.9 1.5 convolution_bitcast_fusion.14
  236.6 1.5 convolution_bitcast_fusion.15
  242.2 4.4 dynamic_update_slice.10
  257.8 1.5 convolution_bitcast_fusion.13
  260.1 1.5 convolution_bitcast_fusion.14
  263.9 1.5 convolution_bitcast_fusion.15
  269.4 4.4 dynamic_update_slice.10
  273.8 8.2 %copy.114 = f32[2,2,640,640]{3,2,1,0:T(8,128)} copy(f32[2,2,640,640]{2,3,1,0:T(8,128)} %get-tuple-element.206) | data formatting | bytes 13107200 | tf_op jit(solution)/shard_map/while | solution.py:187
  283.1 1.9 collective-permute-start.4
  285.0 8.0 %collective-permute-done.4 = f32[2,2,64,640]{3,2,1,0:T(8,128)S(1)} collective-permute-done((f32[2,2,64,640]{3,2,1,0:T(8,128)S(1)}, f32[2,2,64,640]{3,2,1,0:T(8,128)S(1)}, u32[]{:S(2)}, u32[]{:S(2)}) %collective-permute-start.4) | collective-permute-done | bytes 655392 | tf_op jit(solution)/shard_map/ppermute | solution.py:16
  293.1 2.3 slice_add_fusion.7
  295.3 1.5 collective-permute-start.5
  296.8 4.2 slice.281
  301.4 7.1 %collective-permute-done.5 = f32[2,2,64,640]{3,2,1,0:T(8,128)S(1)} collective-permute-done((f32[2,2,64,640]{3,2,1,0:T(8,128)}, f32[2,2,64,640]{3,2,1,0:T(8,128)S(1)}, u32[]{:S(2)}, u32[]{:S(2)}) %collective-permute-start.5) | collective-permute-done | bytes 655392 | tf_op jit(solution)/shard_map/ppermute | solution.py:19
  308.5 2.0 slice_add_fusion.6
  310.5 1.5 copy.119
  312.0 2.0 pad_maximum_fusion.6
  314.0 14.0 %collective-permute-start.6 = (f32[2,2,512,64]{2,3,1,0:T(8,128)}, f32[2,2,512,64]{2,3,1,0:T(8,128)}, u32[]{:S(2)}, u32[]{:S(2)}) collective-permute-start(f32[2,2,512,64]{2,3,1,0:T(8,128)} %pad_maximum_fusion.6), channel_id=1, source_target_pairs={{0,1},{1,2},{2,3},{3,4},{4,5},{5,6},{6,7},{8,9},{9,10},{10,11},{11... | collective-permute-start | bytes 1572872 | tf_op jit(solution)/shard_map/ppermute | solution.py:16
  328.9 66.6 %all-reduce.3.cloned.1.call-done = f32[4,2,128,128]{3,2,1,0:T(8,128)} async-done(((f32[4,2,128,128]{3,2,1,0:T(8,128)}), f32[4,2,128,128]{3,2,1,0:T(8,128)}) %all-reduce.3.cloned.1.call-update) | async-done | bytes 524304 | tf_op jit(solution)/shard_map/psum | solution.py:212
  395.6 2.7 maximum_add_fusion.3
  399.6 36.1 %all-reduce.5.cloned.1.call-done = f32[4,2,128,128]{3,2,1,0:T(8,128)} async-done(((f32[4,2,128,128]{3,2,1,0:T(8,128)}), f32[4,2,128,128]{3,2,1,0:T(8,128)}) %all-reduce.5.cloned.1.call-update) | async-done | bytes 524304 | tf_op jit(solution)/shard_map/psum | solution.py:212
  435.7 1.8 multiply_reduce_fusion
  438.2 2.6 divide_subtract_fusion
  441.4 3.9 pad_maximum_fusion.1
  445.7 1.8 copy-done.2
  447.4 1.7 maximum_add_fusion.2
  449.2 3.0 fusion.85
  452.1 5.2 %copy.122 = f32[2,2,512,512]{3,2,1,0:T(8,128)} copy(f32[2,2,512,512]{2,3,1,0:T(8,128)} %fusion.85) | data formatting | bytes 8388608
  (358 shorter events, 130.0 us)
Async XLA Ops:
  7.2 2.1 copy-start
  10.3 43.0 %all-to-all-start = ((bf16[8,128,128]{2,1,0:T(8,128)(2,1)}), bf16[8,128,128]{2,1,0:T(8,128)(2,1)}, u32[]{:S(2)}, u32[]{:S(2)}) async-start(bf16[8,128,128]{2,1,0:T(8,128)(2,1)} %copy.108), calls=%async_computation | async-start | bytes 524288 | tf_op jit(solution)/shard_map/all_to_all | solution.py:154
  16.7 378.8 %all-reduce.3.cloned.1.call-start = ((), (), s32[]{:S(2)}) async-start(), calls=%async_computation.1 | async-start | bytes 1048576 | tf_op jit(solution)/shard_map/psum | solution.py:212
  18.0 14.5 %collective-permute-start = (f32[2,2,64,512]{3,2,1,0:T(8,128)S(1)}, f32[2,2,64,512]{3,2,1,0:T(8,128)S(1)}, u32[]{:S(2)}, u32[]{:S(2)}) collective-permute-start(f32[2,2,64,512]{3,2,1,0:T(8,128)S(1)} %get-tuple-element.545), channel_id=1, source_target_pairs={{0,8},{8,16},{16,24},{1,9},{9,17},{17,25},{2,10},{10,18},{18,26},{... | collective-permute-start | bytes 1572872 | tf_op jit(solution)/shard_map/ppermute | solution.py:16
  21.9 14.9 %collective-permute-start.1 = (f32[2,2,64,512]{3,2,1,0:T(8,128)S(1)}, f32[2,2,64,512]{3,2,1,0:T(8,128)S(1)}, u32[]{:S(2)}, u32[]{:S(2)}) collective-permute-start(f32[2,2,64,512]{3,2,1,0:T(8,128)S(1)} %get-tuple-element.546), channel_id=1, source_target_pairs={{8,0},{16,8},{24,16},{9,1},{17,9},{25,17},{10,2},{18,10},{26,18},{... | collective-permute-start | bytes 1572872 | tf_op jit(solution)/shard_map/ppermute | solution.py:19
  29.6 0.6 copy-start.8
  29.8 0.6 copy-start.10
  29.9 0.6 copy-start.12
  37.1 6.3 %copy-start.9 = (bf16[128,128]{1,0:T(8,128)(2,1)S(1)}, bf16[128,128]{1,0:T(8,128)(2,1)}, u32[]{:S(2)}) copy-start(bf16[128,128]{1,0:T(8,128)(2,1)} %copy-done.8) | copy-start | bytes 98308
  37.2 6.3 %copy-start.11 = (bf16[128,128]{1,0:T(8,128)(2,1)S(1)}, bf16[128,128]{1,0:T(8,128)(2,1)}, u32[]{:S(2)}) copy-start(bf16[128,128]{1,0:T(8,128)(2,1)} %copy-done.10) | copy-start | bytes 98308
  37.2 6.3 %copy-start.13 = (bf16[128,128]{1,0:T(8,128)(2,1)S(1)}, bf16[128,128]{1,0:T(8,128)(2,1)}, u32[]{:S(2)}) copy-start(bf16[128,128]{1,0:T(8,128)(2,1)} %copy-done.12) | copy-start | bytes 98308
  37.2 6.3 %copy-start.14 = (pred[4,2]{0,1:T(4,128)(4,1)S(1)}, pred[4,2]{0,1:T(4,128)(4,1)}, u32[]{:S(2)}) copy-start(pred[4,2]{0,1:T(4,128)(4,1)} %reduce_or.9) | copy-start | bytes 28
  37.2 6.3 %copy-start.5 = (f32[4,2,128,128]{3,2,1,0:T(8,128)S(1)}, f32[4,2,128,128]{3,2,1,0:T(8,128)}, u32[]{:S(2)}) copy-start(f32[4,2,128,128]{3,2,1,0:T(8,128)} %param.8) | copy-start | bytes 1572868
  40.0 6.6 %collective-permute-start.2 = (f32[2,2,640,64]{2,3,1,0:T(8,128)}, f32[2,2,640,64]{2,3,1,0:T(8,128)}, u32[]{:S(2)}, u32[]{:S(2)}) collective-permute-start(f32[2,2,640,64]{2,3,1,0:T(8,128)} %get-tuple-element.543), channel_id=1, source_target_pairs={{0,1},{1,2},{2,3},{3,4},{4,5},{5,6},{6,7},{8,9},{9,10},{10,11},{11... | collective-permute-start | bytes 1966088 | tf_op jit(solution)/shard_map/ppermute | solution.py:16
  42.1 5.2 %collective-permute-start.3 = (f32[2,2,640,64]{2,3,1,0:T(8,128)}, f32[2,2,640,64]{2,3,1,0:T(8,128)}, u32[]{:S(2)}, u32[]{:S(2)}) collective-permute-start(f32[2,2,640,64]{2,3,1,0:T(8,128)} %get-tuple-element.544), channel_id=1, source_target_pairs={{1,0},{2,1},{3,2},{4,3},{5,4},{6,5},{7,6},{9,8},{10,9},{11,10},{12... | collective-permute-start | bytes 1966088 | tf_op jit(solution)/shard_map/ppermute | solution.py:19
  53.3 3.2 copy-start.15
  75.3 2.3 copy-start.4
  102.5 2.3 copy-start.4
  129.5 2.3 copy-start.4
  156.7 2.3 copy-start.4
  183.9 2.3 copy-start.4
  211.1 2.3 copy-start.4
  238.2 2.3 copy-start.4
  265.5 2.3 copy-start.4
  283.1 9.9 %collective-permute-start.4 = (f32[2,2,64,640]{3,2,1,0:T(8,128)S(1)}, f32[2,2,64,640]{3,2,1,0:T(8,128)S(1)}, u32[]{:S(2)}, u32[]{:S(2)}) collective-permute-start(f32[2,2,64,640]{3,2,1,0:T(8,128)S(1)} %slice.455), channel_id=1, source_target_pairs={{0,8},{8,16},{16,24},{1,9},{9,17},{17,25},{2,10},{10,18},{18,26},{... | collective-permute-start | bytes 1966088 | tf_op jit(solution)/shard_map/ppermute | solution.py:16
  295.3 13.1 %collective-permute-start.5 = (f32[2,2,64,640]{3,2,1,0:T(8,128)}, f32[2,2,64,640]{3,2,1,0:T(8,128)S(1)}, u32[]{:S(2)}, u32[]{:S(2)}) collective-permute-start(f32[2,2,64,640]{3,2,1,0:T(8,128)} %get-tuple-element.542), channel_id=1, source_target_pairs={{8,0},{16,8},{24,16},{9,1},{17,9},{25,17},{10,2},{18,10},{26,18},{... | collective-permute-start | bytes 1966088 | tf_op jit(solution)/shard_map/ppermute | solution.py:19
  314.0 81.6 %collective-permute-start.6 = (f32[2,2,512,64]{2,3,1,0:T(8,128)}, f32[2,2,512,64]{2,3,1,0:T(8,128)}, u32[]{:S(2)}, u32[]{:S(2)}) collective-permute-start(f32[2,2,512,64]{2,3,1,0:T(8,128)} %pad_maximum_fusion.6), channel_id=1, source_target_pairs={{0,1},{1,2},{2,3},{3,4},{4,5},{5,6},{6,7},{8,9},{9,10},{10,11},{11... | collective-permute-start | bytes 1572872 | tf_op jit(solution)/shard_map/ppermute | solution.py:16
  328.9 106.8 %all-reduce.5.cloned.1.call-start = ((), (), s32[]{:S(2)}) async-start(), calls=%async_computation.2 | async-start | bytes 1048576 | tf_op jit(solution)/shard_map/psum | solution.py:212
  395.5 42.7 %copy-start.6 = (f32[4,2,128,128]{3,2,1,0:T(8,128)S(1)}, f32[4,2,128,128]{3,2,1,0:T(8,128)}, u32[]{:S(2)}) copy-start(f32[4,2,128,128]{3,2,1,0:T(8,128)} %param.8) | copy-start | bytes 1572868
  398.3 47.4 %collective-permute-start.7 = (f32[2,2,512,64]{2,3,1,0:T(8,128)}, f32[2,2,512,64]{2,3,1,0:T(8,128)}, u32[]{:S(2)}, u32[]{:S(2)}) collective-permute-start(f32[2,2,512,64]{2,3,1,0:T(8,128)} %get-tuple-element.540), channel_id=1, source_target_pairs={{1,0},{2,1},{3,2},{4,3},{5,4},{6,5},{7,6},{9,8},{10,9},{11,10},{12... | collective-permute-start | bytes 1572872 | tf_op jit(solution)/shard_map/ppermute | solution.py:19
  445.3 2.1 copy-start.2
  445.6 3.5 copy-start.3
  445.7 3.5 copy-start.7
  449.1 8.2 %copy-start.1 = (bf16[8,128,128]{2,1,0:T(8,128)(2,1)S(1)}, bf16[8,128,128]{2,1,0:T(8,128)(2,1)}, u32[]{:S(2)}) copy-start(bf16[8,128,128]{2,1,0:T(8,128)(2,1)} %param.9) | copy-start | bytes 786436
Sparse Core Ops, SparseCore 0:
  329.0 66.4 all-reduce.2
  397.9 37.8 all-reduce.4
